TPU v7x, 32 devices: a whole 2x2x4 slice. The times are simulated.
32 devices in a mesh: ctx: 8 (over y, x, core), rec: 4 (over z).
Axes of the slice: x: 2, y: 2, z: 4, core: 2. Of those that a mesh axis runs over, the one named last changes fastest.
Arguments:
- queries: bfloat16 [4, 1024, 4096], P('rec', 'ctx'), may hold values from -6 to 6
- out_grads: bfloat16 [4, 1024, 4096], P('rec', 'ctx'), may hold values from -6 to 6
- log_sums: float32 [4, 32, 1024], P('rec', None, 'ctx'), may hold values from 1.5 to 4
- deltas: float32 [4, 32, 1024], P('rec', None, 'ctx'), may hold values from -6 to 6
- keys: bfloat16 [1024, 256], P('ctx'), may hold values from -6 to 6
- values: bfloat16 [1024, 256], P('ctx'), may hold values from -0.5 to 0.5
- doc_ids: int32 [4, 8], P('rec'), may hold values from 0 to 3, never falling along the last dimension, each value on 1 to 4 neighbouring positions
Outputs:
- query_grads: bfloat16 [4, 1024, 4096], P('rec', 'ctx')
- key_grads: bfloat16 [1024, 256], P(('ctx', 'rec'))
- value_grads: bfloat16 [1024, 256], P(('ctx', 'rec'))
Inputs may be any that keep to these rules, and one draw needn't show every extreme that they name: `doc_ids`: in each row the numbers never fall, start at 0, each document spans 1 to 4 blocks and some document spans exactly 4 blocks.
All inputs are finite; a program needn't handle non-finite values.
Results may differ from a plain program's by a relative error of at most 0.0062.
Values may be sent and summed in bfloat16 or wider, within the bound.
A program may use at most 64 MiB of HBM per device.

v0:
```python
import jax
import jax.numpy as jnp
from jax import lax
from jax.sharding import PartitionSpec as P

HD = 128
MAXSPAN = 4


def shifted(block, axis, distance):
    devices = range(lax.axis_size(axis))
    route = [(i - distance, i) for i in devices if i - distance in devices]
    return lax.ppermute(block, axis, route)


def from_behind(shard, axis, by):
    peers = lax.axis_size(axis)
    return lax.ppermute(shard, axis, [(i, (i + by) % peers) for i in range(peers)])


def tile_terms(
    query_block, grad_block, sums_block, delta_block, key_block, value_block, query_index, key_index
):
    rows = query_block.shape[0]
    key_heads = key_block.shape[1] // HD
    group = query_block.shape[1] // (key_heads * HD)
    scale = HD ** (-0.5)
    query_heads = query_block.reshape(rows, key_heads, group, HD)
    grad_heads = grad_block.reshape(rows, key_heads, group, HD)
    key_split = key_block.reshape(rows, key_heads, HD)
    value_split = value_block.reshape(rows, key_heads, HD)
    sums_heads = sums_block.reshape(key_heads, group, rows)
    delta_heads = delta_block.reshape(key_heads, group, rows)
    positions = jnp.arange(rows, dtype=jnp.int32)
    query_pos = query_index * rows + positions
    key_pos = key_index * rows + positions
    causal = key_pos[None, :] <= query_pos[:, None]
    scores = (
        jnp.einsum("qkgd,skd->kgqs", query_heads, key_split, preferred_element_type=jnp.float32)
        * scale
    )
    probs = jnp.where(causal, jnp.exp(scores - sums_heads[..., None]), 0.0)
    dprobs = jnp.einsum(
        "qkgd,skd->kgqs", grad_heads, value_split, preferred_element_type=jnp.float32
    )
    dscores = probs * (dprobs - delta_heads[..., None])
    probs_b = probs.astype(jnp.bfloat16)
    dscores_b = dscores.astype(jnp.bfloat16)
    value_grad = jnp.einsum(
        "kgqs,qkgd->skd", probs_b, grad_heads, preferred_element_type=jnp.float32
    ).reshape(rows, key_heads * HD)
    key_grad = (
        jnp.einsum(
            "kgqs,qkgd->skd", dscores_b, query_heads, preferred_element_type=jnp.float32
        ).reshape(rows, key_heads * HD)
        * scale
    )
    query_grad = (
        jnp.einsum(
            "kgqs,skd->qkgd", dscores_b, key_split, preferred_element_type=jnp.float32
        ).reshape(rows, -1)
        * scale
    )
    return (query_grad, key_grad, value_grad)


def guarded(
    active,
    query_block,
    grad_block,
    sums_block,
    delta_block,
    key_block,
    value_block,
    query_index,
    key_index,
):
    rows = query_block.shape[0]

    def compute():
        return tile_terms(
            query_block,
            grad_block,
            sums_block,
            delta_block,
            key_block,
            value_block,
            query_index,
            key_index,
        )

    def nothing():
        return (
            jnp.zeros((rows, query_block.shape[1]), jnp.float32),
            jnp.zeros((rows, key_block.shape[1]), jnp.float32),
            jnp.zeros((rows, key_block.shape[1]), jnp.float32),
        )

    return lax.cond(active, compute, nothing)


def per_device(queries, out_grads, log_sums, deltas, keys, values, doc_ids):
    blocks = lax.axis_size("ctx")
    mine = lax.axis_index("ctx")
    ids = doc_ids[0]
    order = jnp.arange(blocks, dtype=jnp.int32)
    first = jnp.min(jnp.where(ids[:, None] == ids[None, :], order[None, :], blocks), axis=1)
    query_here = queries[0]
    grad_here = out_grads[0]
    sums_here = log_sums[0]
    delta_here = deltas[0]
    start_terms = guarded(
        first[mine] <= mine, query_here, grad_here, sums_here, delta_here, keys, values, mine, mine
    )

    def advance(step, carry):
        pair, partial_value, query_grad = carry
        pair = shifted((pair[0], pair[1]), "ctx", 1)
        partial_value = from_behind((partial_value[0], partial_value[1]), "ctx", 1)
        source = mine - step
        active = source >= first[mine]
        terms = guarded(
            active, query_here, grad_here, sums_here, delta_here, pair[0], pair[1], mine, source
        )
        return (
            pair,
            (partial_value[0] + terms[1], partial_value[1] + terms[2]),
            query_grad + terms[0],
        )

    carry = ((keys, values), (start_terms[1], start_terms[2]), start_terms[0])
    pair, partial_value, query_grad = lax.fori_loop(1, MAXSPAN, advance, carry)
    key_part, value_part = from_behind((partial_value[0], partial_value[1]), "ctx", 1 - MAXSPAN)
    summed = (
        lax.psum_scatter(key_part, "rec", scatter_dimension=0, tiled=True),
        lax.psum_scatter(value_part, "rec", scatter_dimension=0, tiled=True),
    )
    return (
        query_grad[None].astype(jnp.bfloat16),
        summed[0].astype(jnp.bfloat16),
        summed[1].astype(jnp.bfloat16),
    )


def solution(mesh):
    return jax.shard_map(
        per_device,
        mesh=mesh,
        in_specs=(
            P("rec", "ctx", None),
            P("rec", "ctx", None),
            P("rec", None, "ctx"),
            P("rec", None, "ctx"),
            P("ctx", None),
            P("ctx", None),
            P("rec", None),
        ),
        out_specs=(P("rec", "ctx", None), P(("ctx", "rec"), None), P(("ctx", "rec"), None)),
        check_vma=False,
    )
```

profile of v0, /device:TPU:2, one launch (start us, length us, event | category | flops | bytes accessed | tf_op | source)
XLA Modules:
  0.0 131.6 jit_solution(92026165462905907)
XLA Ops:
  7.2 0.9 copy.120
  8.1 0.9 select_reduce_fusion
  9.1 0.6 dynamic_slice.10
  10.4 1.0 copy.50
  11.4 1.6 %copy.51 = bf16[1,128,4096]{1,2,0:T(8,128)(2,1)S(1)} copy(bf16[1,128,4096]{2,1,0:T(8,128)(2,1)} %param.13) | data formatting | bytes 2097152 | tf_op jit(solution)/shard_map/while | solution.py:132
  13.0 1.3 copy.52
  14.3 8.2 %conditional.2 = (f32[128,4096]{0,1:T(8,128)}, f32[128,256]{0,1:T(8,128)}, f32[128,256]{0,1:T(8,128)}) conditional(s32[]{:T(128)} %convert_element_type.36, () %tuple.45, (s32[]{:T(128)}, bf16[128,256]{1,0:T(8,128)(2,1)S(1)}, bf16[1,128,4096]{2,1,0:T(8,128)(2,1)}, f32[1,32,128]{2,1,0:T(8,128)S(1)}, bf16[128,256]{1,0:T(8,128)(2,1)S(1)}, ...), branch_computations={%region_1.2_spmd, %region_2.3_spmd} | conditional | flops 675332224 | bytes 20710440 | solution.py:99
  14.6 0.7 copy.49
  15.3 1.6 %copy.48 = bf16[1,128,4096]{1,2,0:T(8,128)(2,1)S(1)} copy(bf16[1,128,4096]{2,1,0:T(8,128)(2,1)} %get-tuple-element.362) | data formatting | bytes 2097152 | tf_op jit(solution)/shard_map
  17.5 1.1 fusion.5
  18.6 1.2 fusion.1
  19.8 1.1 fusion.4
  20.8 1.8 %convolution_multiply_fusion = f32[2,16,128,128]{2,3,1,0:T(8,128)} fusion(bf16[128,2,128,1]{0,2,3,1:T(8,128)(2,1)S(1)} %bitcast.126, bf16[2,16,128,128]{2,3,1,0:T(8,128)(2,1)S(1)} %fusion.1), kind=kOutput, calls=%fused_computation.6 | convolution fusion | flops 134742016 | bytes 3211264 | tf_op jit(solution)/shard_map/cond/branch_1_fun/kgqs,skd->qkgd/dot_general | solution.py:59
  22.6 50.7 %while.23 = (s32[]{:T(128)}, bf16[128,256]{0,1:T(8,128)(2,1)S(1)}, bf16[128,256]{1,0:T(8,128)(2,1)S(1)}, f32[128,256]{0,1:T(8,128)}, f32[128,256]{0,1:T(8,128)},...) while((s32[]{:T(128)}, bf16[128,256]{0,1:T(8,128)(2,1)S(1)}, ...), condition=%wide.region_6.7_spmd, body=%wide.region_3.6_spmd.sunk | while | flops 675922176 | bytes 29493708 | solution.py:132
  22.6 1.6 %collective-permute-start.3 = (f32[128,256]{0,1:T(8,128)}, f32[128,256]{0,1:T(8,128)}, u32[]{:S(2)}, u32[]{:S(2)}) collective-permute-start(f32[128,256]{0,1:T(8,128)} %get-tuple-element.513), channel_id=1, source_target_pairs={{0,4},{4,8},{8,12},{12,16},{16,20},{20,24},{24,28},{28,0},{1,5},{5... | collective-permute-start | bytes 393224 | tf_op jit(solution)/shard_map/while/body/eval_jaxpr/ppermute | solution.py:18
  24.2 1.9 %collective-permute-start.1 = (bf16[128,256]{1,0:T(8,128)(2,1)S(1)}, bf16[128,256]{1,0:T(8,128)(2,1)S(1)}, u32[]{:S(2)}, u32[]{:S(2)}) collective-permute-start(bf16[128,256]{1,0:T(8,128)(2,1)S(1)} %get-tuple-element.511), channel_id=1, source_target_pairs={{0,4},{4,8},{8,12},{12,16},{16,20},{20,24},{24,28},{1,5},{5,9},{9,... | collective-permute-start | bytes 196616 | tf_op jit(solution)/shard_map/while/body/eval_jaxpr/ppermute | solution.py:13
  26.1 3.5 %collective-permute-start = (bf16[128,256]{0,1:T(8,128)(2,1)S(1)}, bf16[128,256]{0,1:T(8,128)(2,1)S(1)}, u32[]{:S(2)}, u32[]{:S(2)}) collective-permute-start(bf16[128,256]{0,1:T(8,128)(2,1)S(1)} %get-tuple-element.510), channel_id=1, source_target_pairs={{0,4},{4,8},{8,12},{12,16},{16,20},{20,24},{24,28},{1,5},{5,9},{9,... | collective-permute-start | bytes 196616 | tf_op jit(solution)/shard_map/while/body/eval_jaxpr/ppermute | solution.py:13
  30.3 1.4 %collective-permute-done = bf16[128,256]{0,1:T(8,128)(2,1)S(1)} collective-permute-done((bf16[128,256]{0,1:T(8,128)(2,1)S(1)}, bf16[128,256]{0,1:T(8,128)(2,1)S(1)}, u32[]{:S(2)}, u32[]{:S(2)}) %collective-permute-start) | collective-permute-done | bytes 65568 | tf_op jit(solution)/shard_map/while/body/eval_jaxpr/ppermute | solution.py:13
  31.7 3.7 %conditional.4 = (f32[128,4096]{0,1:T(8,128)S(1)}, f32[128,256]{0,1:T(8,128)S(1)}, f32[128,256]{0,1:T(8,128)S(1)}) conditional(s32[]{:T(128)} %convert_element_type.49, () %tuple.64, (s32[]{:T(128)}, s32[]{:T(128)}, bf16[128,256]{0,1:T(8,128)(2,1)S(1)}, bf16[1,128,4096]{1,2,0:T(8,128)(2,1)S(1)}, f32[1,32,128]{2,1,0:T(8,128)S(1)}, ...), branch_computations={%region_4.4_spmd, %region_5.5_spmd} | conditional | flops 675332352 | bytes 20580436 | solution.py:99
  33.4 1.2 fusion.9
  35.4 3.1 %add.110 = f32[128,4096]{0,1:T(8,128)} add(f32[128,4096]{0,1:T(8,128)} %get-tuple-element.514, f32[128,4096]{0,1:T(8,128)S(1)} %get-tuple-element.483) | non-fusion elementwise | flops 524288 | bytes 6291456 | tf_op jit(solution)/shard_map/while/body/eval_jaxpr/add | solution.py:128
  38.6 1.6 %add.108 = f32[128,256]{0,1:T(8,128)} add(f32[128,256]{0,1:T(8,128)} %collective-permute-done.2, f32[128,256]{0,1:T(8,128)S(1)} %get-tuple-element.481) | non-fusion elementwise | flops 32768 | bytes 393216 | tf_op jit(solution)/shard_map/while/body/eval_jaxpr/add | solution.py:127
  40.1 1.6 %add.109 = f32[128,256]{0,1:T(8,128)} add(f32[128,256]{0,1:T(8,128)} %collective-permute-done.3, f32[128,256]{0,1:T(8,128)S(1)} %get-tuple-element.482) | non-fusion elementwise | flops 32768 | bytes 393216 | tf_op jit(solution)/shard_map/while/body/eval_jaxpr/add | solution.py:127
  41.7 1.9 %collective-permute-start.1 = (bf16[128,256]{1,0:T(8,128)(2,1)S(1)}, bf16[128,256]{1,0:T(8,128)(2,1)S(1)}, u32[]{:S(2)}, u32[]{:S(2)}) collective-permute-start(bf16[128,256]{1,0:T(8,128)(2,1)S(1)} %get-tuple-element.511), channel_id=1, source_target_pairs={{0,4},{4,8},{8,12},{12,16},{16,20},{20,24},{24,28},{1,5},{5,9},{9,... | collective-permute-start | bytes 196616 | tf_op jit(solution)/shard_map/while/body/eval_jaxpr/ppermute | solution.py:13
  43.6 3.5 %collective-permute-start = (bf16[128,256]{0,1:T(8,128)(2,1)S(1)}, bf16[128,256]{0,1:T(8,128)(2,1)S(1)}, u32[]{:S(2)}, u32[]{:S(2)}) collective-permute-start(bf16[128,256]{0,1:T(8,128)(2,1)S(1)} %get-tuple-element.510), channel_id=1, source_target_pairs={{0,4},{4,8},{8,12},{12,16},{16,20},{20,24},{24,28},{1,5},{5,9},{9,... | collective-permute-start | bytes 196616 | tf_op jit(solution)/shard_map/while/body/eval_jaxpr/ppermute | solution.py:13
  48.4 0.8 collective-permute-done
  49.3 3.7 %conditional.4 = (f32[128,4096]{0,1:T(8,128)S(1)}, f32[128,256]{0,1:T(8,128)S(1)}, f32[128,256]{0,1:T(8,128)S(1)}) conditional(s32[]{:T(128)} %convert_element_type.49, () %tuple.64, (s32[]{:T(128)}, s32[]{:T(128)}, bf16[128,256]{0,1:T(8,128)(2,1)S(1)}, bf16[1,128,4096]{1,2,0:T(8,128)(2,1)S(1)}, f32[1,32,128]{2,1,0:T(8,128)S(1)}, ...), branch_computations={%region_4.4_spmd, %region_5.5_spmd} | conditional | flops 675332352 | bytes 20580436 | solution.py:99
  50.9 1.2 fusion.9
  53.0 3.1 %add.110 = f32[128,4096]{0,1:T(8,128)} add(f32[128,4096]{0,1:T(8,128)} %get-tuple-element.514, f32[128,4096]{0,1:T(8,128)S(1)} %get-tuple-element.483) | non-fusion elementwise | flops 524288 | bytes 6291456 | tf_op jit(solution)/shard_map/while/body/eval_jaxpr/add | solution.py:128
  56.1 1.6 %add.108 = f32[128,256]{0,1:T(8,128)} add(f32[128,256]{0,1:T(8,128)} %collective-permute-done.2, f32[128,256]{0,1:T(8,128)S(1)} %get-tuple-element.481) | non-fusion elementwise | flops 32768 | bytes 393216 | tf_op jit(solution)/shard_map/while/body/eval_jaxpr/add | solution.py:127
  57.7 1.6 %add.109 = f32[128,256]{0,1:T(8,128)} add(f32[128,256]{0,1:T(8,128)} %collective-permute-done.3, f32[128,256]{0,1:T(8,128)S(1)} %get-tuple-element.482) | non-fusion elementwise | flops 32768 | bytes 393216 | tf_op jit(solution)/shard_map/while/body/eval_jaxpr/add | solution.py:127
  59.3 1.9 %collective-permute-start.1 = (bf16[128,256]{1,0:T(8,128)(2,1)S(1)}, bf16[128,256]{1,0:T(8,128)(2,1)S(1)}, u32[]{:S(2)}, u32[]{:S(2)}) collective-permute-start(bf16[128,256]{1,0:T(8,128)(2,1)S(1)} %get-tuple-element.511), channel_id=1, source_target_pairs={{0,4},{4,8},{8,12},{12,16},{16,20},{20,24},{24,28},{1,5},{5,9},{9,... | collective-permute-start | bytes 196616 | tf_op jit(solution)/shard_map/while/body/eval_jaxpr/ppermute | solution.py:13
  61.2 1.9 %collective-permute-start = (bf16[128,256]{0,1:T(8,128)(2,1)S(1)}, bf16[128,256]{0,1:T(8,128)(2,1)S(1)}, u32[]{:S(2)}, u32[]{:S(2)}) collective-permute-start(bf16[128,256]{0,1:T(8,128)(2,1)S(1)} %get-tuple-element.510), channel_id=1, source_target_pairs={{0,4},{4,8},{8,12},{12,16},{16,20},{20,24},{24,28},{1,5},{5,9},{9,... | collective-permute-start | bytes 196616 | tf_op jit(solution)/shard_map/while/body/eval_jaxpr/ppermute | solution.py:13
  63.8 2.2 %collective-permute-done.1 = bf16[128,256]{1,0:T(8,128)(2,1)S(1)} collective-permute-done((bf16[128,256]{1,0:T(8,128)(2,1)S(1)}, bf16[128,256]{1,0:T(8,128)(2,1)S(1)}, u32[]{:S(2)}, u32[]{:S(2)}) %collective-permute-start.1) | collective-permute-done | bytes 65568 | tf_op jit(solution)/shard_map/while/body/eval_jaxpr/ppermute | solution.py:13
  66.0 0.8 collective-permute-done
  67.0 3.1 %add.110 = f32[128,4096]{0,1:T(8,128)} add(f32[128,4096]{0,1:T(8,128)} %get-tuple-element.514, f32[128,4096]{0,1:T(8,128)S(1)} %get-tuple-element.483) | non-fusion elementwise | flops 524288 | bytes 6291456 | tf_op jit(solution)/shard_map/while/body/eval_jaxpr/add | solution.py:128
  70.2 1.6 %add.108 = f32[128,256]{0,1:T(8,128)} add(f32[128,256]{0,1:T(8,128)} %collective-permute-done.2, f32[128,256]{0,1:T(8,128)S(1)} %get-tuple-element.481) | non-fusion elementwise | flops 32768 | bytes 393216 | tf_op jit(solution)/shard_map/while/body/eval_jaxpr/add | solution.py:127
  71.7 1.6 %add.109 = f32[128,256]{0,1:T(8,128)} add(f32[128,256]{0,1:T(8,128)} %collective-permute-done.3, f32[128,256]{0,1:T(8,128)S(1)} %get-tuple-element.482) | non-fusion elementwise | flops 32768 | bytes 393216 | tf_op jit(solution)/shard_map/while/body/eval_jaxpr/add | solution.py:127
  73.3 1.0 copy.55
  74.4 5.4 %collective-permute-done.5 = f32[128,256]{1,0:T(8,128)S(1)} collective-permute-done((f32[128,256]{1,0:T(8,128)S(1)}, f32[128,256]{1,0:T(8,128)S(1)}, u32[]{:S(2)}, u32[]{:S(2)}) %collective-permute-start.5) | collective-permute-done | bytes 131104 | tf_op jit(solution)/shard_map/ppermute | solution.py:18
  80.5 1.0 copy.54
  81.5 5.4 %collective-permute-done.4 = f32[128,256]{1,0:T(8,128)S(1)} collective-permute-done((f32[128,256]{1,0:T(8,128)S(1)}, f32[128,256]{1,0:T(8,128)S(1)}, u32[]{:S(2)}, u32[]{:S(2)}) %collective-permute-start.4) | collective-permute-done | bytes 131104 | tf_op jit(solution)/shard_map/ppermute | solution.py:18
  86.9 0.7 copy-done.5
  87.6 2.5 %copy.53 = bf16[128,4096]{1,0:T(8,128)(2,1)} copy(f32[128,4096]{0,1:T(8,128)} %get-tuple-element.338) | data formatting | bytes 3145728 | tf_op jit(solution)/shard_map/while | solution.py:132
  90.1 13.3 %reduce-scatter.5.cloned.1.call-done = f32[32,256]{1,0:T(8,128)} async-done(((f32[128,256]{1,0:T(8,128)}), f32[32,256]{1,0:T(8,128)}) %reduce-scatter.5.cloned.1.call-update) | async-done | bytes 32784 | tf_op jit(solution)/shard_map/reduce_scatter | solution.py:136
  103.5 1.4 %convert_element_type.40 = bf16[32,256]{1,0:T(8,128)(2,1)} convert(f32[32,256]{1,0:T(8,128)} %reduce-scatter.5.cloned.1.call-done) | non-fusion elementwise | flops 8192 | bytes 49152 | tf_op jit(solution)/shard_map/convert_element_type | solution.py:141
  104.8 18.5 %reduce-scatter.3.cloned.1.call-done = f32[32,256]{1,0:T(8,128)} async-done(((f32[128,256]{1,0:T(8,128)}), f32[32,256]{1,0:T(8,128)}) %reduce-scatter.3.cloned.1.call-update) | async-done | bytes 32784 | tf_op jit(solution)/shard_map/reduce_scatter | solution.py:135
  123.4 1.4 %convert_element_type.39 = bf16[32,256]{1,0:T(8,128)(2,1)} convert(f32[32,256]{1,0:T(8,128)} %reduce-scatter.3.cloned.1.call-done) | non-fusion elementwise | flops 8192 | bytes 49152 | tf_op jit(solution)/shard_map/convert_element_type | solution.py:140
  (61 shorter events, 7.7 us)
Async XLA Ops:
  7.2 5.9 %copy-start.1 = (bf16[1,128,4096]{2,1,0:T(8,128)(2,1)S(1)}, bf16[1,128,4096]{2,1,0:T(8,128)(2,1)}, u32[]{:S(2)}) copy-start(bf16[1,128,4096]{2,1,0:T(8,128)(2,1)} %param.14) | copy-start | bytes 3145732
  7.2 96.3 %reduce-scatter.5.cloned.1.call-start = ((), (), s32[]{:S(2)}) async-start(), calls=%async_computation.3 | async-start | bytes 163840 | tf_op jit(solution)/shard_map/reduce_scatter | solution.py:136
  11.3 3.0 %copy-start.2 = (f32[1,32,128]{2,1,0:T(8,128)S(1)}, f32[1,32,128]{2,1,0:T(8,128)}, u32[]{:S(2)}) copy-start(f32[1,32,128]{2,1,0:T(8,128)} %param.15) | copy-start | bytes 49156
  11.4 3.0 %copy-start.3 = (bf16[128,256]{1,0:T(8,128)(2,1)S(1)}, bf16[128,256]{1,0:T(8,128)(2,1)}, u32[]{:S(2)}) copy-start(bf16[128,256]{1,0:T(8,128)(2,1)} %param.17) | copy-start | bytes 196612
  22.6 16.0 %collective-permute-start.2 = (f32[128,256]{0,1:T(8,128)}, f32[128,256]{0,1:T(8,128)}, u32[]{:S(2)}, u32[]{:S(2)}) collective-permute-start(f32[128,256]{0,1:T(8,128)} %get-tuple-element.512), channel_id=1, source_target_pairs={{0,4},{4,8},{8,12},{12,16},{16,20},{20,24},{24,28},{28,0},{1,5},{5... | collective-permute-start | bytes 393224 | tf_op jit(solution)/shard_map/while/body/eval_jaxpr/ppermute | solution.py:18
  22.6 17.5 %collective-permute-start.3 = (f32[128,256]{0,1:T(8,128)}, f32[128,256]{0,1:T(8,128)}, u32[]{:S(2)}, u32[]{:S(2)}) collective-permute-start(f32[128,256]{0,1:T(8,128)} %get-tuple-element.513), channel_id=1, source_target_pairs={{0,4},{4,8},{8,12},{12,16},{16,20},{20,24},{24,28},{28,0},{1,5},{5... | collective-permute-start | bytes 393224 | tf_op jit(solution)/shard_map/while/body/eval_jaxpr/ppermute | solution.py:18
  24.2 6.1 %collective-permute-start.1 = (bf16[128,256]{1,0:T(8,128)(2,1)S(1)}, bf16[128,256]{1,0:T(8,128)(2,1)S(1)}, u32[]{:S(2)}, u32[]{:S(2)}) collective-permute-start(bf16[128,256]{1,0:T(8,128)(2,1)S(1)} %get-tuple-element.511), channel_id=1, source_target_pairs={{0,4},{4,8},{8,12},{12,16},{16,20},{20,24},{24,28},{1,5},{5,9},{9,... | collective-permute-start | bytes 196616 | tf_op jit(solution)/shard_map/while/body/eval_jaxpr/ppermute | solution.py:13
  26.1 5.6 %collective-permute-start = (bf16[128,256]{0,1:T(8,128)(2,1)S(1)}, bf16[128,256]{0,1:T(8,128)(2,1)S(1)}, u32[]{:S(2)}, u32[]{:S(2)}) collective-permute-start(bf16[128,256]{0,1:T(8,128)(2,1)S(1)} %get-tuple-element.510), channel_id=1, source_target_pairs={{0,4},{4,8},{8,12},{12,16},{16,20},{20,24},{24,28},{1,5},{5,9},{9,... | collective-permute-start | bytes 196616 | tf_op jit(solution)/shard_map/while/body/eval_jaxpr/ppermute | solution.py:13
  31.7 1.2 copy-start
  41.7 14.4 %collective-permute-start.2 = (f32[128,256]{0,1:T(8,128)}, f32[128,256]{0,1:T(8,128)}, u32[]{:S(2)}, u32[]{:S(2)}) collective-permute-start(f32[128,256]{0,1:T(8,128)} %get-tuple-element.512), channel_id=1, source_target_pairs={{0,4},{4,8},{8,12},{12,16},{16,20},{20,24},{24,28},{28,0},{1,5},{5... | collective-permute-start | bytes 393224 | tf_op jit(solution)/shard_map/while/body/eval_jaxpr/ppermute | solution.py:18
  41.7 16.0 %collective-permute-start.3 = (f32[128,256]{0,1:T(8,128)}, f32[128,256]{0,1:T(8,128)}, u32[]{:S(2)}, u32[]{:S(2)}) collective-permute-start(f32[128,256]{0,1:T(8,128)} %get-tuple-element.513), channel_id=1, source_target_pairs={{0,4},{4,8},{8,12},{12,16},{16,20},{20,24},{24,28},{28,0},{1,5},{5... | collective-permute-start | bytes 393224 | tf_op jit(solution)/shard_map/while/body/eval_jaxpr/ppermute | solution.py:18
  41.7 6.7 %collective-permute-start.1 = (bf16[128,256]{1,0:T(8,128)(2,1)S(1)}, bf16[128,256]{1,0:T(8,128)(2,1)S(1)}, u32[]{:S(2)}, u32[]{:S(2)}) collective-permute-start(bf16[128,256]{1,0:T(8,128)(2,1)S(1)} %get-tuple-element.511), channel_id=1, source_target_pairs={{0,4},{4,8},{8,12},{12,16},{16,20},{20,24},{24,28},{1,5},{5,9},{9,... | collective-permute-start | bytes 196616 | tf_op jit(solution)/shard_map/while/body/eval_jaxpr/ppermute | solution.py:13
  43.6 5.6 %collective-permute-start = (bf16[128,256]{0,1:T(8,128)(2,1)S(1)}, bf16[128,256]{0,1:T(8,128)(2,1)S(1)}, u32[]{:S(2)}, u32[]{:S(2)}) collective-permute-start(bf16[128,256]{0,1:T(8,128)(2,1)S(1)} %get-tuple-element.510), channel_id=1, source_target_pairs={{0,4},{4,8},{8,12},{12,16},{16,20},{20,24},{24,28},{1,5},{5,9},{9,... | collective-permute-start | bytes 196616 | tf_op jit(solution)/shard_map/while/body/eval_jaxpr/ppermute | solution.py:13
  49.3 1.2 copy-start
  59.3 10.9 %collective-permute-start.2 = (f32[128,256]{0,1:T(8,128)}, f32[128,256]{0,1:T(8,128)}, u32[]{:S(2)}, u32[]{:S(2)}) collective-permute-start(f32[128,256]{0,1:T(8,128)} %get-tuple-element.512), channel_id=1, source_target_pairs={{0,4},{4,8},{8,12},{12,16},{16,20},{20,24},{24,28},{28,0},{1,5},{5... | collective-permute-start | bytes 393224 | tf_op jit(solution)/shard_map/while/body/eval_jaxpr/ppermute | solution.py:18
  59.3 12.4 %collective-permute-start.3 = (f32[128,256]{0,1:T(8,128)}, f32[128,256]{0,1:T(8,128)}, u32[]{:S(2)}, u32[]{:S(2)}) collective-permute-start(f32[128,256]{0,1:T(8,128)} %get-tuple-element.513), channel_id=1, source_target_pairs={{0,4},{4,8},{8,12},{12,16},{16,20},{20,24},{24,28},{28,0},{1,5},{5... | collective-permute-start | bytes 393224 | tf_op jit(solution)/shard_map/while/body/eval_jaxpr/ppermute | solution.py:18
  59.3 6.7 %collective-permute-start.1 = (bf16[128,256]{1,0:T(8,128)(2,1)S(1)}, bf16[128,256]{1,0:T(8,128)(2,1)S(1)}, u32[]{:S(2)}, u32[]{:S(2)}) collective-permute-start(bf16[128,256]{1,0:T(8,128)(2,1)S(1)} %get-tuple-element.511), channel_id=1, source_target_pairs={{0,4},{4,8},{8,12},{12,16},{16,20},{20,24},{24,28},{1,5},{5,9},{9,... | collective-permute-start | bytes 196616 | tf_op jit(solution)/shard_map/while/body/eval_jaxpr/ppermute | solution.py:13
  61.2 5.6 %collective-permute-start = (bf16[128,256]{0,1:T(8,128)(2,1)S(1)}, bf16[128,256]{0,1:T(8,128)(2,1)S(1)}, u32[]{:S(2)}, u32[]{:S(2)}) collective-permute-start(bf16[128,256]{0,1:T(8,128)(2,1)S(1)} %get-tuple-element.510), channel_id=1, source_target_pairs={{0,4},{4,8},{8,12},{12,16},{16,20},{20,24},{24,28},{1,5},{5,9},{9,... | collective-permute-start | bytes 196616 | tf_op jit(solution)/shard_map/while/body/eval_jaxpr/ppermute | solution.py:13
  74.3 5.4 %collective-permute-start.5 = (f32[128,256]{1,0:T(8,128)S(1)}, f32[128,256]{1,0:T(8,128)S(1)}, u32[]{:S(2)}, u32[]{:S(2)}) collective-permute-start(f32[128,256]{1,0:T(8,128)S(1)} %copy.55), channel_id=1, source_target_pairs={{0,20},{4,24},{8,28},{12,0},{16,4},{20,8},{24,12},{28,16},{1,21},{... | collective-permute-start | bytes 393224 | tf_op jit(solution)/shard_map/ppermute | solution.py:18
  79.7 0.6 copy-start.4
  80.4 43.0 %reduce-scatter.3.cloned.1.call-start = ((), (), s32[]{:S(2)}) async-start(), calls=%async_computation.2 | async-start | bytes 163840 | tf_op jit(solution)/shard_map/reduce_scatter | solution.py:135
  81.5 5.4 %collective-permute-start.4 = (f32[128,256]{1,0:T(8,128)S(1)}, f32[128,256]{1,0:T(8,128)S(1)}, u32[]{:S(2)}, u32[]{:S(2)}) collective-permute-start(f32[128,256]{1,0:T(8,128)S(1)} %copy.54), channel_id=1, source_target_pairs={{0,20},{4,24},{8,28},{12,0},{16,4},{20,8},{24,12},{28,16},{1,21},{... | collective-permute-start | bytes 393224 | tf_op jit(solution)/shard_map/ppermute | solution.py:18
  86.9 0.7 copy-start.5
Sparse Core Ops, SparseCore 0:
  80.5 22.9 reduce-scatter.4
  105.7 17.6 reduce-scatter.2
where the time goes:
time: 134 us; the launch traced here: 132 us
  waiting for transfers between devices  48.5 us (36%)
  other arithmetic  22.7 us (17%)
  starting transfers between devices  16.5 us (12%)
  local copies, waits for them, and re-layouts  15 us (11%)
  between operations  14.8 us (11%)
  matrix products  11.8 us (9%)
  loops' own time  2.32 us (2%)
    reduce_scatter x1, waiting for transfers between devices, per_device(): lax.psum_scatter(key_part, 'rec', scatter_dimension=0, tiled=True)  18.5 us
    ppermute x6, starting transfers between devices, shifted(): return lax.ppermute(block, axis, route)  14.7 us
    reduce_scatter x1, waiting for transfers between devices, per_device(): lax.psum_scatter(value_part, 'rec', scatter_dimension=0, tiled=True)  13.3 us
    ppermute x8, waiting for transfers between devices, from_behind(): lax.ppermute(shard, axis, [(i, (i + by) % peers) for i in range(peers)])  10.8 us
    add x3, other arithmetic, advance(): query_grad + terms[0]  9.41 us
    while x6, local copies, waits for them, and re-layouts, per_device(): pair, partial_value, query_grad = lax.fori_loop(1, MAXSPAN, advance, carry)  8.45 us
    ppermute x6, waiting for transfers between devices, shifted(): return lax.ppermute(block, axis, route)  5.8 us
    add x3, other arithmetic, advance(): partial_value[1] + terms[2]  4.72 us
  transfers between devices with their start and end apart: 16, of which 9 were waited for; matrix products, arithmetic and copies ran while one was open for 19% of the time, Pallas kernels for 0%

commit v1 on v0

v1 whole, which is shorter than its diff:
```python
import functools
import math

import jax
import jax.numpy as jnp
from jax import lax
from jax.experimental import pallas as pl
from jax.experimental.pallas import tpu as pltpu
from jax.sharding import PartitionSpec as P

HD = 128
MAXSPAN = 4
HEADS = 4
BACK = MAXSPAN - 1
MESH = pl.DeviceIdType.MESH
FAR = 1e30


def kernel(
    q_hbm, g_hbm, sums_ref, delta_ref, k_hbm, v_hbm, ids_ref,
    dq_hbm, dk_ref, dv_ref,
    q_buf, g_buf, kv, key_t, ds_buf, dq_buf, acc, part, landed, total, r_send, r_land,
    load_sem, own_sem, kv_send, kv_recv, g_send, g_recv, rec_send, rec_recv, out_sem,
):
    peers = lax.axis_size("ctx")
    recs = lax.axis_size("rec")
    mine = lax.axis_index("ctx")
    rec = lax.axis_index("rec")
    rows = q_buf.shape[0]
    key_heads = kv.shape[0]
    group = q_buf.shape[1] // (key_heads * HD)
    chunks = group // HEADS
    wide = HEADS * HD
    scale = HD ** (-0.5)
    fold = scale * math.log2(math.e)
    share = rows // recs

    def own_copy(g, which):
        source = (k_hbm, v_hbm)[which]
        return pltpu.make_async_copy(
            source.at[:, pl.ds(g * HD, HD)],
            kv.at[g, which, pl.ds(0, rows), :],
            own_sem.at[g, which],
        )

    def lanes(g, c):
        return pl.ds(pl.multiple_of((g * chunks + c) * wide, wide), wide)

    def load(g, c, which):
        source, target = ((q_hbm, q_buf), (g_hbm, g_buf))[which]
        return pltpu.make_async_copy(
            source.at[0, :, lanes(g, c)], target.at[:, lanes(g, c)], load_sem.at[g, c, which]
        )

    def kv_copy(g, k):
        return pltpu.make_async_remote_copy(
            src_ref=kv.at[g, :, pl.ds(0, rows), :],
            dst_ref=kv.at[g, :, pl.ds(k * rows, rows), :],
            send_sem=kv_send.at[g, k - 1],
            recv_sem=kv_recv.at[g, k - 1],
            device_id={"ctx": lax.rem(mine + k, peers)},
            device_id_type=MESH,
        )

    def grad_copy(g, k):
        return pltpu.make_async_remote_copy(
            src_ref=part.at[g, k - 1],
            dst_ref=landed.at[g, k - 1],
            send_sem=g_send.at[g, k - 1],
            recv_sem=g_recv.at[g, k - 1],
            device_id={"ctx": lax.rem(mine - k + peers, peers)},
            device_id_type=MESH,
        )

    def rec_copy(g, j):
        target = lax.rem(rec + j, recs)
        return pltpu.make_async_remote_copy(
            src_ref=r_send.at[g, :, pl.ds(pl.multiple_of(target * share, share), share), :],
            dst_ref=r_land.at[g, j - 1],
            send_sem=rec_send.at[g, j - 1],
            recv_sem=rec_recv.at[g, j - 1],
            device_id={"rec": target},
            device_id_type=MESH,
        )

    for g in range(key_heads):
        for which in range(2):
            own_copy(g, which).start()
    for g in range(key_heads):
        for c in range(chunks):
            for which in range(2):
                load(g, c, which).start()

    barrier = pltpu.get_barrier_semaphore()
    for k in range(1, MAXSPAN):
        for other in (lax.rem(mine + k, peers), lax.rem(mine - k + peers, peers)):
            pl.semaphore_signal(barrier, inc=1, device_id={"ctx": other}, device_id_type=MESH)
    for j in range(1, recs):
        pl.semaphore_signal(
            barrier, inc=1, device_id={"rec": lax.rem(rec + j, recs)}, device_id_type=MESH
        )
    for k in range(1, MAXSPAN):
        @pl.when(mine < k)
        def _():
            kv[:, :, pl.ds(k * rows, rows), :] = jnp.zeros((key_heads, 2, rows, HD), kv.dtype)

        @pl.when(mine + k >= peers)
        def _():
            landed[:, k - 1] = jnp.zeros((key_heads, 2, rows, HD), landed.dtype)
    acc[...] = jnp.zeros_like(acc)
    pl.semaphore_wait(barrier, 2 * BACK + recs - 1)

    for g in range(key_heads):
        for which in range(2):
            own_copy(g, which).wait()
        for k in range(1, MAXSPAN):
            @pl.when(mine + k < peers)
            def _():
                kv_copy(g, k).start()

    here = ids_ref[0, mine]
    far = [jnp.float32(0.0)]
    for k in range(1, MAXSPAN):
        same = (ids_ref[0, jnp.maximum(mine - k, 0)] == here) & (mine >= k)
        far.append(jnp.where(same, 0.0, FAR).astype(jnp.float32))

    def heads_down(ref, g, c):
        first = (g * chunks + c) * HEADS
        return jnp.concatenate(
            [ref[:, pl.ds(pl.multiple_of((first + i) * HD, HD), HD)] for i in range(HEADS)], axis=0
        )

    def heads_along(ref, g, c):
        first = (g * chunks + c) * HEADS
        return jnp.concatenate([ref[0, pl.ds(first + i, 1), :] for i in range(HEADS)], axis=1)

    inner = (((1,), (1,)), ((), ()))

    def sweep(g, tiles, loads, finish):
        @pl.loop(0, chunks)
        def _(c):
            if loads:
                for which in range(2):
                    load(g, c, which).wait()
            query = heads_down(q_buf, g, c)
            grad = heads_down(g_buf, g, c)
            sums = heads_along(sums_ref, g, c) * math.log2(math.e)
            delta = heads_along(delta_ref, g, c)
            for k in tiles:
                at = pl.ds(k * rows, rows)
                scores = lax.dot_general(
                    kv[g, 0, at, :], query, inner, preferred_element_type=jnp.float32
                )
                dprobs = lax.dot_general(
                    kv[g, 1, at, :], grad, inner, preferred_element_type=jnp.float32
                )
                probs = jnp.exp2(scores * fold - (sums + far[k]))
                if k == 0:
                    u = lax.broadcasted_iota(jnp.int32, (rows, wide), 0)
                    t = lax.broadcasted_iota(jnp.int32, (rows, wide), 1) & (rows - 1)
                    probs = jnp.where(u <= t, probs, 0.0)
                ds = (probs * (dprobs - delta)).astype(jnp.bfloat16)
                probs = probs.astype(jnp.bfloat16)
                ds_buf[at, lanes(g, c)] = ds
                acc[g, 0, at, :] += jnp.dot(ds, query, preferred_element_type=jnp.float32)
                acc[g, 1, at, :] += jnp.dot(probs, grad, preferred_element_type=jnp.float32)
            if finish:
                dq = jnp.dot(
                    key_t[g], ds_buf[:, lanes(g, c)], preferred_element_type=jnp.float32
                ) * scale
                for i in range(HEADS):
                    at = pl.ds(pl.multiple_of(((g * chunks + c) * HEADS + i) * HD, HD), HD)
                    dq_buf[:, at] = dq[:, i * rows:(i + 1) * rows].T.astype(dq_buf.dtype)
                pltpu.make_async_copy(
                    dq_buf.at[:, lanes(g, c)], dq_hbm.at[0, :, lanes(g, c)], out_sem.at[g, c]
                ).start()

    def turn(g, k):
        at = pl.ds(k * rows, rows)
        key_t[g, :, k * rows:(k + 1) * rows] = kv[g, 0, at, :].T

    def arrive(g):
        for k in range(1, MAXSPAN):
            @pl.when(mine >= k)
            def _():
                kv_copy(g, k).wait_recv()
            turn(g, k)

    def leave(g):
        for k in range(1, MAXSPAN):
            part[g, k - 1] = acc[g, :, k * rows:(k + 1) * rows, :].astype(part.dtype)

            @pl.when(mine >= k)
            def _():
                grad_copy(g, k).start()

    def across(g):
        whole = acc[g, :, 0:rows, :]
        for k in range(1, MAXSPAN):
            @pl.when(mine + k < peers)
            def _():
                grad_copy(g, k).wait_recv()
        for k in range(1, MAXSPAN):
            whole = whole + landed[g, k - 1].astype(jnp.float32)
        total[g] = whole
        r_send[g] = whole.astype(r_send.dtype)
        for j in range(1, recs):
            rec_copy(g, j).start()

    def close(g):
        whole = total[g, :, pl.ds(pl.multiple_of(rec * share, share), share), :]
        for j in range(1, recs):
            rec_copy(g, j).wait_recv()
            whole = whole + r_land[g, j - 1].astype(jnp.float32)
        dk_ref[:, g * HD:(g + 1) * HD] = (whole[0] * scale).astype(dk_ref.dtype)
        dv_ref[:, g * HD:(g + 1) * HD] = whole[1].astype(dv_ref.dtype)

    off = tuple(range(1, MAXSPAN))
    last = key_heads - 1
    for g in range(key_heads):
        turn(g, 0)
    for g in range(last):
        sweep(g, (0,), True, False)
    for g in range(last):
        arrive(g)
        sweep(g, off, False, True)
        leave(g)
    arrive(last)
    sweep(last, off, True, False)
    leave(last)
    for g in range(last):
        across(g)
    sweep(last, (0,), False, True)
    across(last)
    for g in range(key_heads):
        close(g)
    for g in range(key_heads):
        for c in range(chunks):
            pltpu.make_async_copy(
                dq_buf.at[:, lanes(g, c)], dq_hbm.at[0, :, lanes(g, c)], out_sem.at[g, c]
            ).wait()
        for k in range(1, MAXSPAN):
            @pl.when(mine + k < peers)
            def _():
                kv_copy(g, k).wait_send()

            @pl.when(mine >= k)
            def _():
                grad_copy(g, k).wait_send()
        for j in range(1, recs):
            rec_copy(g, j).wait_send()


def per_device(queries, out_grads, log_sums, deltas, keys, values, doc_ids):
    recs = lax.axis_size("rec")
    rows, width = queries.shape[1:]
    key_heads = keys.shape[1] // HD
    chunks = width // (key_heads * HD * HEADS)
    span = MAXSPAN * rows
    half = jnp.bfloat16
    dma = pltpu.SemaphoreType.DMA
    anywhere = pl.BlockSpec(memory_space=pl.ANY)
    vmem = pl.BlockSpec(memory_space=pltpu.VMEM)
    return pl.pallas_call(
        kernel,
        out_shape=(
            jax.ShapeDtypeStruct(queries.shape, half),
            jax.ShapeDtypeStruct((rows // recs, keys.shape[1]), half),
            jax.ShapeDtypeStruct((rows // recs, keys.shape[1]), half),
        ),
        in_specs=[
            anywhere, anywhere, vmem, vmem, anywhere, anywhere,
            pl.BlockSpec(memory_space=pltpu.SMEM),
        ],
        out_specs=(anywhere, vmem, vmem),
        scratch_shapes=[
            pltpu.VMEM((rows, width), half),
            pltpu.VMEM((rows, width), half),
            pltpu.VMEM((key_heads, 2, span, HD), half),
            pltpu.VMEM((key_heads, HD, span), half),
            pltpu.VMEM((span, width), half),
            pltpu.VMEM((rows, width), half),
            pltpu.VMEM((key_heads, 2, span, HD), jnp.float32),
            pltpu.VMEM((key_heads, BACK, 2, rows, HD), half),
            pltpu.VMEM((key_heads, BACK, 2, rows, HD), half),
            pltpu.VMEM((key_heads, 2, rows, HD), jnp.float32),
            pltpu.VMEM((key_heads, 2, rows, HD), half),
            pltpu.VMEM((key_heads, max(recs - 1, 1), 2, rows // recs, HD), half),
            dma((key_heads, chunks, 2)),
            dma((key_heads, 2)),
            dma((key_heads, BACK)),
            dma((key_heads, BACK)),
            dma((key_heads, BACK)),
            dma((key_heads, BACK)),
            dma((key_heads, max(recs - 1, 1))),
            dma((key_heads, max(recs - 1, 1))),
            dma((key_heads, chunks)),
        ],
        compiler_params=pltpu.CompilerParams(
            collective_id=0, has_side_effects=True, vmem_limit_bytes=48 * 1024 * 1024
        ),
    )(queries, out_grads, log_sums, deltas, keys, values, doc_ids)


def solution(mesh):
    return jax.shard_map(
        per_device,
        mesh=mesh,
        in_specs=(
            P("rec", "ctx", None),
            P("rec", "ctx", None),
            P("rec", None, "ctx"),
            P("rec", None, "ctx"),
            P("ctx", None),
            P("ctx", None),
            P("rec", None),
        ),
        out_specs=(P("rec", "ctx", None), P(("ctx", "rec"), None), P(("ctx", "rec"), None)),
        check_vma=False,
    )
```

time: 134 us -> 39.4 us (0.29); the launches traced: 132 us -> 39 us
  waiting for transfers between devices: 48.5 us -> 0 us
  Pallas kernels: 0 us -> 30 us
  other arithmetic: 22.7 us -> 0 us
  starting transfers between devices: 16.5 us -> 0 us
  between operations: 14.8 us -> 0.66 us
  matrix products: 11.8 us -> 0 us
  local copies, waits for them, and re-layouts: 15 us -> 8.39 us
  loops' own time: 2.32 us -> 0 us
    reduce_scatter x2 -> x0, waiting for transfers between devices: 31.9 us -> none  [the longest x1 18.5 us: per_device(): lax.psum_scatter(key_part, 'rec', scatter_dimension=0, tiled=True)]
    pallas_call x0 -> x1, Pallas kernels: none -> 30 us  [per_device(): pl.pallas_call(kernel, out_shape=(jax.ShapeDtypeStruct(queries.shape, hal...]
    add x12 -> x0, other arithmetic: 18.8 us -> none  [the longest x3 9.41 us: advance(): query_grad + terms[0]]
    ppermute x14 -> x0, waiting for transfers between devices: 16.6 us -> none  [the longest x8 10.8 us: from_behind(): lax.ppermute(shard, axis, [(i, (i + by) % peers) for i in range(peers)])]
    ppermute x14 -> x0, starting transfers between devices: 16.4 us -> none  [the longest x6 14.7 us: shifted(): return lax.ppermute(block, axis, route)]
    dot_general x15 -> x0, matrix products: 11.8 us -> none  [the longest x3 3.47 us: tile_terms(): jnp.einsum('qkgd,skd->kgqs', grad_heads, value_split, preferred_element_t...]
    while x12 -> x0, local copies, waits for them, and re-layouts: 8.48 us -> none  [the longest x6 8.45 us: per_device(): pair, partial_value, query_grad = lax.fori_loop(1, MAXSPAN, advance, carry)]
    unnamed x11 -> x17, local copies, waits for them, and re-layouts: 2.23 us -> 8.39 us
  transfers between devices with their start and end apart: 16 -> 0, of which waited for: 9 -> 0; matrix products, arithmetic and copies ran while one was open for 19% -> 0% of each run, Pallas kernels for 0% -> 0%
where the time goes in v1:
time: 39.4 us; the launch traced here: 39 us
  Pallas kernels  30 us (76%)
  local copies, waits for them, and re-layouts  8.39 us (21%)
  between operations  0.66 us (2%)
    pallas_call x1, Pallas kernels, per_device(): pl.pallas_call(kernel, out_shape=(jax.ShapeDtypeStruct(queries.shape, hal...  30 us
    unnamed x17, local copies, waits for them, and re-layouts  8.39 us

profile of v1, /device:TPU:2, one launch (start us, length us, event | category | flops | bytes accessed | tf_op | source)
XLA Modules:
  0.0 39.0 jit_solution(4802439777284258037)
XLA Ops:
  0.6 0.0 copy-start
  0.6 1.2 %copy-done = bf16[1,128,4096]{2,1,0:T(8,128)(2,1)S(1)} copy-done((bf16[1,128,4096]{2,1,0:T(8,128)(2,1)S(1)}, bf16[1,128,4096]{2,1,0:T(8,128)(2,1)}, u32[]{:S(2)}) %copy-start) | copy-done | bytes 1048600
  1.9 0.0 copy-start.1
  1.9 1.2 %copy-done.1 = bf16[1,128,4096]{2,1,0:T(8,128)(2,1)S(1)} copy-done((bf16[1,128,4096]{2,1,0:T(8,128)(2,1)S(1)}, bf16[1,128,4096]{2,1,0:T(8,128)(2,1)}, u32[]{:S(2)}) %copy-start.1) | copy-done | bytes 1048600
  3.1 0.0 copy-start.2
  3.1 0.8 %copy-done.2 = bf16[128,256]{1,0:T(8,128)(2,1)S(1)} copy-done((bf16[128,256]{1,0:T(8,128)(2,1)S(1)}, bf16[128,256]{1,0:T(8,128)(2,1)}, u32[]{:S(2)}) %copy-start.2) | copy-done | bytes 65560
  3.9 0.0 copy-start.3
  3.9 0.8 %copy-done.3 = bf16[128,256]{1,0:T(8,128)(2,1)S(1)} copy-done((bf16[128,256]{1,0:T(8,128)(2,1)S(1)}, bf16[128,256]{1,0:T(8,128)(2,1)}, u32[]{:S(2)}) %copy-start.3) | copy-done | bytes 65560
  4.8 0.0 copy-start.4
  4.8 0.7 %copy-done.4 = f32[1,32,128]{2,1,0:T(8,128)S(1)} copy-done((f32[1,32,128]{2,1,0:T(8,128)S(1)}, f32[1,32,128]{2,1,0:T(8,128)}, u32[]{:S(2)}) %copy-start.4) | copy-done | bytes 16408
  5.5 0.0 copy-start.5
  5.5 0.7 %copy-done.5 = f32[1,32,128]{2,1,0:T(8,128)S(1)} copy-done((f32[1,32,128]{2,1,0:T(8,128)S(1)}, f32[1,32,128]{2,1,0:T(8,128)}, u32[]{:S(2)}) %copy-start.5) | copy-done | bytes 16408
  6.2 0.0 copy-start.6
  6.2 0.7 %copy-done.6 = s32[1,8]{1,0:T(1,128)S(1)} copy-done((s32[1,8]{1,0:T(1,128)S(1)}, s32[1,8]{1,0:T(1,128)}, u32[]{:S(2)}) %copy-start.6) | copy-done | bytes 56
  6.9 30.0 %shard_map.94 = (bf16[1,128,4096]{2,1,0:T(8,128)(2,1)S(1)}, bf16[32,256]{1,0:T(8,128)(2,1)S(1)}, bf16[32,256]{1,0:T(8,128)(2,1)S(1)}) custom-call(bf16[1,128,4096]{2,1,0:T(8,128)(2,1)S(1)} %copy-done, bf16[1,128,4096]{2,1,0:T(8,128)(2,1)S(1)} %copy-done.1, f32[1,32,128]{2,1,0:T(8,128)S(1)} %copy-done.4, f32[1,32,128]{2,1,0:T(8,128)S(1)} %copy-done.5, ...), custom_call_target="tpu_custom_call" | custom-call | tf_op jit(solution)/shard_map/pallas_call | solution.py:264
  36.9 1.0 %copy.13 = bf16[1,128,4096]{2,1,0:T(8,128)(2,1)} copy(bf16[1,128,4096]{2,1,0:T(8,128)(2,1)S(1)} %get-tuple-element.6) | data formatting | bytes 2097152
  37.8 0.6 %copy.14 = bf16[32,256]{1,0:T(8,128)(2,1)} copy(bf16[32,256]{1,0:T(8,128)(2,1)S(1)} %get-tuple-element.7) | data formatting | bytes 32768
  38.4 0.6 %copy.15 = bf16[32,256]{1,0:T(8,128)(2,1)} copy(bf16[32,256]{1,0:T(8,128)(2,1)S(1)} %get-tuple-element.8) | data formatting | bytes 32768
Async XLA Ops:
  0.6 1.2 %copy-start = (bf16[1,128,4096]{2,1,0:T(8,128)(2,1)S(1)}, bf16[1,128,4096]{2,1,0:T(8,128)(2,1)}, u32[]{:S(2)}) copy-start(bf16[1,128,4096]{2,1,0:T(8,128)(2,1)} %q_hbm.1) | copy-start | bytes 3145732
  1.9 1.2 %copy-start.1 = (bf16[1,128,4096]{2,1,0:T(8,128)(2,1)S(1)}, bf16[1,128,4096]{2,1,0:T(8,128)(2,1)}, u32[]{:S(2)}) copy-start(bf16[1,128,4096]{2,1,0:T(8,128)(2,1)} %g_hbm.1) | copy-start | bytes 3145732
  3.1 0.8 %copy-start.2 = (bf16[128,256]{1,0:T(8,128)(2,1)S(1)}, bf16[128,256]{1,0:T(8,128)(2,1)}, u32[]{:S(2)}) copy-start(bf16[128,256]{1,0:T(8,128)(2,1)} %k_hbm.1) | copy-start | bytes 196612
  3.9 0.8 %copy-start.3 = (bf16[128,256]{1,0:T(8,128)(2,1)S(1)}, bf16[128,256]{1,0:T(8,128)(2,1)}, u32[]{:S(2)}) copy-start(bf16[128,256]{1,0:T(8,128)(2,1)} %v_hbm.1) | copy-start | bytes 196612
  4.8 0.7 %copy-start.4 = (f32[1,32,128]{2,1,0:T(8,128)S(1)}, f32[1,32,128]{2,1,0:T(8,128)}, u32[]{:S(2)}) copy-start(f32[1,32,128]{2,1,0:T(8,128)} %sums_ref.1) | copy-start | bytes 49156
  5.5 0.7 %copy-start.5 = (f32[1,32,128]{2,1,0:T(8,128)S(1)}, f32[1,32,128]{2,1,0:T(8,128)}, u32[]{:S(2)}) copy-start(f32[1,32,128]{2,1,0:T(8,128)} %delta_ref.1) | copy-start | bytes 49156
  6.2 0.7 %copy-start.6 = (s32[1,8]{1,0:T(1,128)S(1)}, s32[1,8]{1,0:T(1,128)}, u32[]{:S(2)}) copy-start(s32[1,8]{1,0:T(1,128)} %ids_ref.1) | copy-start | bytes 100

commit v2 on v1

--- a/solution.py
+++ b/solution.py
@@ -17,10 +17,10 @@
 
 
 def kernel(
-    q_hbm, g_hbm, sums_ref, delta_ref, k_hbm, v_hbm, ids_ref,
+    q_hbm, g_hbm, sums_hbm, delta_hbm, k_hbm, v_hbm, ids_hbm,
     dq_hbm, dk_ref, dv_ref,
-    q_buf, g_buf, kv, key_t, ds_buf, dq_buf, acc, part, landed, total, r_send, r_land,
-    load_sem, own_sem, kv_send, kv_recv, g_send, g_recv, rec_send, rec_recv, out_sem,
+    q_buf, g_buf, sums_ref, delta_ref, ids_ref, kv, key_t, ds_buf, dq_buf, acc, part, landed, total, r_send, r_land,
+    load_sem, own_sem, small_sem, kv_send, kv_recv, g_send, g_recv, rec_send, rec_recv, out_sem,
 ):
     peers = lax.axis_size("ctx")
     recs = lax.axis_size("rec")
@@ -52,6 +52,11 @@
             source.at[0, :, lanes(g, c)], target.at[:, lanes(g, c)], load_sem.at[g, c, which]
         )
 
+    def out_copy(g, c):
+        return pltpu.make_async_copy(
+            dq_buf.at[:, lanes(g, c)], dq_hbm.at[0, :, lanes(g, c)], out_sem.at[g, c]
+        )
+
     def kv_copy(g, k):
         return pltpu.make_async_remote_copy(
             src_ref=kv.at[g, :, pl.ds(0, rows), :],
@@ -86,6 +91,14 @@
     for g in range(key_heads):
         for which in range(2):
             own_copy(g, which).start()
+    small = [
+        pltpu.make_async_copy(source, target, small_sem.at[i])
+        for i, (source, target) in enumerate(
+            ((sums_hbm, sums_ref), (delta_hbm, delta_ref), (ids_hbm, ids_ref))
+        )
+    ]
+    for copy in small:
+        copy.start()
     for g in range(key_heads):
         for c in range(chunks):
             for which in range(2):
@@ -118,6 +131,8 @@
             def _():
                 kv_copy(g, k).start()
 
+    for copy in small:
+        copy.wait()
     here = ids_ref[0, mine]
     far = [jnp.float32(0.0)]
     for k in range(1, MAXSPAN):
@@ -171,9 +186,7 @@
                 for i in range(HEADS):
                     at = pl.ds(pl.multiple_of(((g * chunks + c) * HEADS + i) * HD, HD), HD)
                     dq_buf[:, at] = dq[:, i * rows:(i + 1) * rows].T.astype(dq_buf.dtype)
-                pltpu.make_async_copy(
-                    dq_buf.at[:, lanes(g, c)], dq_hbm.at[0, :, lanes(g, c)], out_sem.at[g, c]
-                ).start()
+                out_copy(g, c).start()
 
     def turn(g, k):
         at = pl.ds(k * rows, rows)
@@ -236,9 +249,7 @@
         close(g)
     for g in range(key_heads):
         for c in range(chunks):
-            pltpu.make_async_copy(
-                dq_buf.at[:, lanes(g, c)], dq_hbm.at[0, :, lanes(g, c)], out_sem.at[g, c]
-            ).wait()
+            out_copy(g, c).wait()
         for k in range(1, MAXSPAN):
             @pl.when(mine + k < peers)
             def _():
@@ -259,7 +270,7 @@
     span = MAXSPAN * rows
     half = jnp.bfloat16
     dma = pltpu.SemaphoreType.DMA
-    anywhere = pl.BlockSpec(memory_space=pl.ANY)
+    far_off = pl.BlockSpec(memory_space=pltpu.HBM)
     vmem = pl.BlockSpec(memory_space=pltpu.VMEM)
     return pl.pallas_call(
         kernel,
@@ -268,14 +279,14 @@
             jax.ShapeDtypeStruct((rows // recs, keys.shape[1]), half),
             jax.ShapeDtypeStruct((rows // recs, keys.shape[1]), half),
         ),
-        in_specs=[
-            anywhere, anywhere, vmem, vmem, anywhere, anywhere,
-            pl.BlockSpec(memory_space=pltpu.SMEM),
-        ],
-        out_specs=(anywhere, vmem, vmem),
+        in_specs=[far_off] * 7,
+        out_specs=(far_off, vmem, vmem),
         scratch_shapes=[
             pltpu.VMEM((rows, width), half),
             pltpu.VMEM((rows, width), half),
+            pltpu.VMEM(log_sums.shape, jnp.float32),
+            pltpu.VMEM(deltas.shape, jnp.float32),
+            pltpu.SMEM(doc_ids.shape, jnp.int32),
             pltpu.VMEM((key_heads, 2, span, HD), half),
             pltpu.VMEM((key_heads, HD, span), half),
             pltpu.VMEM((span, width), half),
@@ -288,6 +299,7 @@
             pltpu.VMEM((key_heads, max(recs - 1, 1), 2, rows // recs, HD), half),
             dma((key_heads, chunks, 2)),
             dma((key_heads, 2)),
+            dma((3,)),
             dma((key_heads, BACK)),
             dma((key_heads, BACK)),
             dma((key_heads, BACK)),
@@ -297,7 +309,7 @@
             dma((key_heads, chunks)),
         ],
         compiler_params=pltpu.CompilerParams(
-            collective_id=0, has_side_effects=True, vmem_limit_bytes=48 * 1024 * 1024
+            collective_id=0, has_side_effects=True, vmem_limit_bytes=67_043_328
         ),
     )(queries, out_grads, log_sums, deltas, keys, values, doc_ids)
 

time: 39.4 us -> 34.1 us (0.87)
  local copies, waits for them, and re-layouts: 8.39 us -> 3.63 us
  Pallas kernels: 30 us -> 29.6 us
    unnamed x17 -> x7, local copies, waits for them, and re-layouts: 8.39 us -> 3.63 us
    pallas_call x1, Pallas kernels: 30 us -> 29.6 us  [per_device(): pl.pallas_call(kernel, out_shape=(jax.ShapeDtypeStruct(queries.shape, hal...]
where the time goes in v2:
time: 34.1 us; the launch traced here: 33.9 us
  Pallas kernels  29.6 us (87%)
  local copies, waits for them, and re-layouts  3.63 us (11%)
  between operations  0.65 us (2%)
    pallas_call x1, Pallas kernels, per_device(): pl.pallas_call(kernel, out_shape=(jax.ShapeDtypeStruct(queries.shape, hal...  29.6 us
    unnamed x7, local copies, waits for them, and re-layouts  3.63 us

profile of v2, /device:TPU:2, one launch (start us, length us, event | category | flops | bytes accessed | tf_op | source)
XLA Modules:
  0.0 33.9 jit_solution(8145091973679934443)
XLA Ops:
  0.6 29.6 %shard_map.94 = (bf16[1,128,4096]{2,1,0:T(8,128)(2,1)}, bf16[32,256]{1,0:T(8,128)(2,1)}, bf16[32,256]{1,0:T(8,128)(2,1)}) custom-call(bf16[1,128,4096]{2,1,0:T(8,128)(2,1)} %q_hbm.1, bf16[1,128,4096]{2,1,0:T(8,128)(2,1)} %g_hbm.1, f32[1,32,128]{2,1,0:T(8,128)} %sums_hbm.1, f32[1,32,128]{2,1,0:T(8,128)} %delta_hbm.1, bf16[128,256]{1,0:T(8,128)(2,1)} %k_hbm.1, ...), custom_call_target="tpu_custom_call" | custom-call | tf_op jit(solution)/shard_map/pallas_call | solution.py:275
  30.2 0.0 copy-start.1
  30.2 2.3 %copy.13 = bf16[1,128,4096]{2,1,0:T(8,128)(2,1)} copy(bf16[1,128,4096]{2,1,0:T(8,128)(2,1)} %get-tuple-element.6) | data formatting | bytes 2097152
  32.5 0.0 copy-done.1
  32.5 0.0 copy-start
  32.5 0.6 %copy.14 = bf16[32,256]{1,0:T(8,128)(2,1)} copy(bf16[32,256]{1,0:T(8,128)(2,1)S(1)} %copy-done.1) | data formatting | bytes 32768
  33.1 0.1 copy-done
  33.3 0.6 %copy.15 = bf16[32,256]{1,0:T(8,128)(2,1)} copy(bf16[32,256]{1,0:T(8,128)(2,1)S(1)} %copy-done) | data formatting | bytes 32768
Async XLA Ops:
  30.2 2.3 %copy-start.1 = (bf16[32,256]{1,0:T(8,128)(2,1)S(1)}, bf16[32,256]{1,0:T(8,128)(2,1)}, u32[]{:S(2)}) copy-start(bf16[32,256]{1,0:T(8,128)(2,1)} %get-tuple-element.7) | copy-start | bytes 49156
  32.5 0.7 %copy-start = (bf16[32,256]{1,0:T(8,128)(2,1)S(1)}, bf16[32,256]{1,0:T(8,128)(2,1)}, u32[]{:S(2)}) copy-start(bf16[32,256]{1,0:T(8,128)(2,1)} %get-tuple-element.8) | copy-start | bytes 49156

commit v3 on v2

--- a/solution.py
+++ b/solution.py
@@ -14,6 +14,7 @@
 BACK = MAXSPAN - 1
 MESH = pl.DeviceIdType.MESH
 FAR = 1e30
+PIECES = 4
 
 
 def kernel(
@@ -151,61 +152,61 @@
 
     inner = (((1,), (1,)), ((), ()))
 
-    def sweep(g, tiles, loads, finish):
+    def sweep(g, k):
+        at = pl.ds(k * rows, rows)
+
         @pl.loop(0, chunks)
         def _(c):
-            if loads:
+            if k == 0:
                 for which in range(2):
                     load(g, c, which).wait()
             query = heads_down(q_buf, g, c)
             grad = heads_down(g_buf, g, c)
-            sums = heads_along(sums_ref, g, c) * math.log2(math.e)
+            sums = heads_along(sums_ref, g, c) * math.log2(math.e) + far[k]
             delta = heads_along(delta_ref, g, c)
-            for k in tiles:
-                at = pl.ds(k * rows, rows)
-                scores = lax.dot_general(
-                    kv[g, 0, at, :], query, inner, preferred_element_type=jnp.float32
-                )
-                dprobs = lax.dot_general(
-                    kv[g, 1, at, :], grad, inner, preferred_element_type=jnp.float32
-                )
-                probs = jnp.exp2(scores * fold - (sums + far[k]))
-                if k == 0:
-                    u = lax.broadcasted_iota(jnp.int32, (rows, wide), 0)
-                    t = lax.broadcasted_iota(jnp.int32, (rows, wide), 1) & (rows - 1)
-                    probs = jnp.where(u <= t, probs, 0.0)
-                ds = (probs * (dprobs - delta)).astype(jnp.bfloat16)
-                probs = probs.astype(jnp.bfloat16)
-                ds_buf[at, lanes(g, c)] = ds
-                acc[g, 0, at, :] += jnp.dot(ds, query, preferred_element_type=jnp.float32)
-                acc[g, 1, at, :] += jnp.dot(probs, grad, preferred_element_type=jnp.float32)
-            if finish:
-                dq = jnp.dot(
-                    key_t[g], ds_buf[:, lanes(g, c)], preferred_element_type=jnp.float32
-                ) * scale
-                for i in range(HEADS):
-                    at = pl.ds(pl.multiple_of(((g * chunks + c) * HEADS + i) * HD, HD), HD)
-                    dq_buf[:, at] = dq[:, i * rows:(i + 1) * rows].T.astype(dq_buf.dtype)
-                out_copy(g, c).start()
+            scores = lax.dot_general(
+                kv[g, 0, at, :], query, inner, preferred_element_type=jnp.float32
+            )
+            dprobs = lax.dot_general(
+                kv[g, 1, at, :], grad, inner, preferred_element_type=jnp.float32
+            )
+            probs = jnp.exp2(scores * fold - sums)
+            if k == 0:
+                u = lax.broadcasted_iota(jnp.int32, (rows, wide), 0)
+                t = lax.broadcasted_iota(jnp.int32, (rows, wide), 1) & (rows - 1)
+                probs = jnp.where(u <= t, probs, 0.0)
+            ds = (probs * (dprobs - delta)).astype(jnp.bfloat16)
+            probs = probs.astype(jnp.bfloat16)
+            ds_buf[at, lanes(g, c)] = ds
+            acc[g, 0, at, :] += jnp.dot(ds, query, preferred_element_type=jnp.float32)
+            acc[g, 1, at, :] += jnp.dot(probs, grad, preferred_element_type=jnp.float32)
+
+    def query_side(g):
+        @pl.loop(0, chunks)
+        def _(c):
+            dq = jnp.dot(
+                key_t[g], ds_buf[:, lanes(g, c)], preferred_element_type=jnp.float32
+            ) * scale
+            for i in range(HEADS):
+                at = pl.ds(pl.multiple_of(((g * chunks + c) * HEADS + i) * HD, HD), HD)
+                dq_buf[:, at] = dq[:, i * rows:(i + 1) * rows].T.astype(dq_buf.dtype)
+            out_copy(g, c).start()
 
     def turn(g, k):
         at = pl.ds(k * rows, rows)
         key_t[g, :, k * rows:(k + 1) * rows] = kv[g, 0, at, :].T
 
-    def arrive(g):
-        for k in range(1, MAXSPAN):
-            @pl.when(mine >= k)
-            def _():
-                kv_copy(g, k).wait_recv()
-            turn(g, k)
-
-    def leave(g):
-        for k in range(1, MAXSPAN):
-            part[g, k - 1] = acc[g, :, k * rows:(k + 1) * rows, :].astype(part.dtype)
-
-            @pl.when(mine >= k)
-            def _():
-                grad_copy(g, k).start()
+    def tile(g, k):
+        @pl.when(mine >= k)
+        def _():
+            kv_copy(g, k).wait_recv()
+        sweep(g, k)
+        part[g, k - 1] = acc[g, :, k * rows:(k + 1) * rows, :].astype(part.dtype)
+
+        @pl.when(mine >= k)
+        def _():
+            grad_copy(g, k).start()
+        turn(g, k)
 
     def across(g):
         whole = acc[g, :, 0:rows, :]
@@ -228,23 +229,19 @@
         dk_ref[:, g * HD:(g + 1) * HD] = (whole[0] * scale).astype(dk_ref.dtype)
         dv_ref[:, g * HD:(g + 1) * HD] = whole[1].astype(dv_ref.dtype)
 
-    off = tuple(range(1, MAXSPAN))
     last = key_heads - 1
     for g in range(key_heads):
+        sweep(g, 0)
         turn(g, 0)
-    for g in range(last):
-        sweep(g, (0,), True, False)
-    for g in range(last):
-        arrive(g)
-        sweep(g, off, False, True)
-        leave(g)
-    arrive(last)
-    sweep(last, off, True, False)
-    leave(last)
+    for g in range(key_heads):
+        order = range(1, MAXSPAN) if g < last else range(BACK, 0, -1)
+        for k in order:
+            tile(g, k)
     for g in range(last):
         across(g)
-    sweep(last, (0,), False, True)
+        query_side(g)
     across(last)
+    query_side(last)
     for g in range(key_heads):
         close(g)
     for g in range(key_heads):
@@ -260,6 +257,24 @@
                 grad_copy(g, k).wait_send()
         for j in range(1, recs):
             rec_copy(g, j).wait_send()
+
+
+def finish(dq_in, dk_in, dv_in, dq_out, dk_out, dv_out, big, dk, dv, into, out):
+    pieces = big.shape[0]
+    depth = big.shape[1]
+    pairs = [
+        (dq_in.at[0, pl.ds(i * depth, depth), :], big.at[i], dq_out.at[0, pl.ds(i * depth, depth), :])
+        for i in range(pieces)
+    ] + [(dk_in, dk, dk_out), (dv_in, dv, dv_out)]
+    ins = [pltpu.make_async_copy(p[0], p[1], into.at[i]) for i, p in enumerate(pairs)]
+    outs = [pltpu.make_async_copy(p[1], p[2], out.at[i]) for i, p in enumerate(pairs)]
+    for copy in ins:
+        copy.start()
+    for arrived, leaving in zip(ins, outs):
+        arrived.wait()
+        leaving.start()
+    for copy in outs:
+        copy.wait()
 
 
 def per_device(queries, out_grads, log_sums, deltas, keys, values, doc_ids):
@@ -272,13 +287,15 @@
     dma = pltpu.SemaphoreType.DMA
     far_off = pl.BlockSpec(memory_space=pltpu.HBM)
     vmem = pl.BlockSpec(memory_space=pltpu.VMEM)
-    return pl.pallas_call(
+    small = (rows // recs, keys.shape[1])
+    shapes = (
+        jax.ShapeDtypeStruct(queries.shape, half),
+        jax.ShapeDtypeStruct(small, half),
+        jax.ShapeDtypeStruct(small, half),
+    )
+    grads = pl.pallas_call(
         kernel,
-        out_shape=(
-            jax.ShapeDtypeStruct(queries.shape, half),
-            jax.ShapeDtypeStruct((rows // recs, keys.shape[1]), half),
-            jax.ShapeDtypeStruct((rows // recs, keys.shape[1]), half),
-        ),
+        out_shape=shapes,
         in_specs=[far_off] * 7,
         out_specs=(far_off, vmem, vmem),
         scratch_shapes=[
@@ -312,6 +329,20 @@
             collective_id=0, has_side_effects=True, vmem_limit_bytes=67_043_328
         ),
     )(queries, out_grads, log_sums, deltas, keys, values, doc_ids)
+    return pl.pallas_call(
+        finish,
+        out_shape=shapes,
+        in_specs=[far_off] * 3,
+        out_specs=(far_off,) * 3,
+        scratch_shapes=[
+            pltpu.VMEM((PIECES, rows // PIECES, width), half),
+            pltpu.VMEM(small, half),
+            pltpu.VMEM(small, half),
+            dma((PIECES + 2,)),
+            dma((PIECES + 2,)),
+        ],
+        compiler_params=pltpu.CompilerParams(vmem_limit_bytes=67_043_328),
+    )(*grads)
 
 
 def solution(mesh):

time: 34.1 us -> 29.5 us (0.87)
  the two profiles are of different devices: /device:TPU:2 before, /device:TPU:3 now
where the time goes in v3:
time: 29.5 us; the launch traced here: 29.4 us
  Pallas kernels  28.7 us (97%)
  between operations  0.64 us (2%)
    pallas_call x1, Pallas kernels, per_device(): pl.pallas_call(kernel, out_shape=shapes, in_specs=[far_off] * 7, out_spec...  26.7 us
    pallas_call x1, Pallas kernels, per_device(): pl.pallas_call(finish, out_shape=shapes, in_specs=[far_off] * 3, out_spec...  2.02 us

profile of v3, /device:TPU:3, one launch (start us, length us, event | category | flops | bytes accessed | tf_op | source)
XLA Modules:
  0.0 29.4 jit_solution(9489884317722237306)
XLA Ops:
  0.6 26.7 %shard_map.94 = (bf16[1,128,4096]{2,1,0:T(8,128)(2,1)}, bf16[32,256]{1,0:T(8,128)(2,1)}, bf16[32,256]{1,0:T(8,128)(2,1)}) custom-call(bf16[1,128,4096]{2,1,0:T(8,128)(2,1)} %q_hbm.1, bf16[1,128,4096]{2,1,0:T(8,128)(2,1)} %g_hbm.1, f32[1,32,128]{2,1,0:T(8,128)} %sums_hbm.1, f32[1,32,128]{2,1,0:T(8,128)} %delta_hbm.1, bf16[128,256]{1,0:T(8,128)(2,1)} %k_hbm.1, ...), custom_call_target="tpu_custom_call" | custom-call | tf_op jit(solution)/shard_map/pallas_call | solution.py:296
  27.4 2.0 %shard_map.95 = (bf16[1,128,4096]{2,1,0:T(8,128)(2,1)}, bf16[32,256]{1,0:T(8,128)(2,1)}, bf16[32,256]{1,0:T(8,128)(2,1)}) custom-call(bf16[1,128,4096]{2,1,0:T(8,128)(2,1)} %get-tuple-element.6.dq_in, bf16[32,256]{1,0:T(8,128)(2,1)} %get-tuple-element.7.dk_in, bf16[32,256]{1,0:T(8,128)(2,1)} %get-tuple-element.8.dv_in), custom_call_target="tpu_custom_call" | custom-call | tf_op jit(solution)/shard_map/pallas_call | solution.py:332

commit v4 on v3

--- a/solution.py
+++ b/solution.py
@@ -10,7 +10,7 @@
 
 HD = 128
 MAXSPAN = 4
-HEADS = 4
+HEADS = 16
 BACK = MAXSPAN - 1
 MESH = pl.DeviceIdType.MESH
 FAR = 1e30

time: 29.5 us -> 26.2 us (0.89)
  the two profiles are of different devices: /device:TPU:3 before, /device:TPU:2 now
where the time goes in v4:
time: 26.2 us; the launch traced here: 25.8 us
  Pallas kernels  25.2 us (96%)
  between operations  0.64 us (2%)
    pallas_call x1, Pallas kernels, per_device(): pl.pallas_call(kernel, out_shape=shapes, in_specs=[far_off] * 7, out_spec...  23.1 us
    pallas_call x1, Pallas kernels, per_device(): pl.pallas_call(finish, out_shape=shapes, in_specs=[far_off] * 3, out_spec...  2.02 us

profile of v4, /device:TPU:2, one launch (start us, length us, event | category | flops | bytes accessed | tf_op | source)
XLA Modules:
  0.0 25.8 jit_solution(4974297834290976339)
XLA Ops:
  0.6 23.1 %shard_map.94 = (bf16[1,128,4096]{2,1,0:T(8,128)(2,1)}, bf16[32,256]{1,0:T(8,128)(2,1)}, bf16[32,256]{1,0:T(8,128)(2,1)}) custom-call(bf16[1,128,4096]{2,1,0:T(8,128)(2,1)} %q_hbm.1, bf16[1,128,4096]{2,1,0:T(8,128)(2,1)} %g_hbm.1, f32[1,32,128]{2,1,0:T(8,128)} %sums_hbm.1, f32[1,32,128]{2,1,0:T(8,128)} %delta_hbm.1, bf16[128,256]{1,0:T(8,128)(2,1)} %k_hbm.1, ...), custom_call_target="tpu_custom_call" | custom-call | tf_op jit(solution)/shard_map/pallas_call | solution.py:296
  23.8 2.0 %shard_map.95 = (bf16[1,128,4096]{2,1,0:T(8,128)(2,1)}, bf16[32,256]{1,0:T(8,128)(2,1)}, bf16[32,256]{1,0:T(8,128)(2,1)}) custom-call(bf16[1,128,4096]{2,1,0:T(8,128)(2,1)} %get-tuple-element.6.dq_in, bf16[32,256]{1,0:T(8,128)(2,1)} %get-tuple-element.7.dk_in, bf16[32,256]{1,0:T(8,128)(2,1)} %get-tuple-element.8.dv_in), custom_call_target="tpu_custom_call" | custom-call | tf_op jit(solution)/shard_map/pallas_call | solution.py:332
